TPU v7x, 32 devices: a whole 2x2x4 slice. The times are simulated.
32 devices in a mesh: blk: 4 (over x, core), grp: 8 (over z, y).
Axes of the slice: x: 2, y: 2, z: 4, core: 2. Of those that a mesh axis runs over, the one named last changes fastest.
Arguments:
- text: bfloat16 [32, 512], P(('blk', 'grp')), may hold values from -20 to 20
- keys: bfloat16 [32, 196, 512], P(('blk', 'grp')), may hold values from -400 to 400
- values: bfloat16 [32, 196, 512], P(('blk', 'grp')), may hold values from -5 to 5
- pair_image: int32 [32], replicated, may hold values from 0 to 31, each once
Outputs:
- caption_loss: float32 [32], P(('blk', 'grp'))
- grad_text: float32 [32, 512], P(('blk', 'grp'))
- grad_keys: float32 [32, 196, 512], P(('blk', 'grp'))
- grad_values: float32 [32, 196, 512], P(('blk', 'grp'))
All inputs are finite; a program needn't handle non-finite values.
Results may differ from a plain program's by a relative error of at most 0.008.
Values may be sent and summed in bfloat16 or wider, within the bound.
A program may use at most 64 MiB of HBM per device.

v0:
```python
import jax
import jax.numpy as jnp
from jax import lax
from jax.sharding import PartitionSpec as P

HEADS = 8
EPS = 1e-06
LOGIT_SCALE = 10.0
LOGIT_BIAS = -1.0


def passed_along(block, axis, distance):
    devices = range(lax.axis_size(axis))
    route = [((i - distance) % len(devices), i) for i in devices]
    return lax.ppermute(block, axis, route)


def image_terms(block_text, normed, tnorm, pairs, image_id, keys_one, values_one):
    count = block_text.shape[0]
    width = block_text.shape[1]
    depth = width // HEADS
    queries = block_text.reshape(count, HEADS, depth)
    patch_keys = keys_one.reshape(-1, HEADS, depth)
    patch_values = values_one.reshape(-1, HEADS, depth)
    scores = jnp.einsum(
        "chd,phd->chp", queries, patch_keys, preferred_element_type=jnp.float32
    ) * depth ** (-0.5)
    weights = jax.nn.softmax(scores, axis=-1)
    attn = weights.astype(jnp.bfloat16)
    pooled = jnp.einsum(
        "chp,phd->chd", attn, patch_values, preferred_element_type=jnp.float32
    ).reshape(count, width)
    pnorm = lax.rsqrt(jnp.mean(pooled * pooled, -1, keepdims=True) + EPS)
    unit = pooled * pnorm
    cosine = jnp.mean(unit * normed, -1)
    logit = LOGIT_SCALE * cosine + LOGIT_BIAS
    label = jnp.where(pairs == image_id, 1.0, -1.0).astype(jnp.float32)
    loss = jax.nn.softplus(-label * logit)
    slope = -label * jax.nn.sigmoid(-label * logit)
    dcos = LOGIT_SCALE / width * slope[:, None]
    dunit = dcos * normed
    dnormed = dcos * unit
    dpool = pnorm * (dunit - unit * jnp.mean(dunit * unit, -1, keepdims=True))
    dout = dpool.astype(jnp.bfloat16).reshape(count, HEADS, depth)
    dattn = jnp.einsum("chd,phd->chp", dout, patch_values, preferred_element_type=jnp.float32)
    grad_v = jnp.einsum("chp,chd->phd", attn, dout, preferred_element_type=jnp.float32).reshape(
        -1, width
    )
    dscore = (
        weights * (dattn - jnp.sum(weights * dattn, -1, keepdims=True)) * depth ** (-0.5)
    ).astype(jnp.bfloat16)
    grad_q = jnp.einsum(
        "chp,phd->chd", dscore, patch_keys, preferred_element_type=jnp.float32
    ).reshape(count, width)
    grad_k = jnp.einsum(
        "chp,chd->phd", dscore, queries, preferred_element_type=jnp.float32
    ).reshape(-1, width)
    grad_x = grad_q + tnorm * (dnormed - normed * jnp.mean(dnormed * normed, -1, keepdims=True))
    return (loss, grad_x, grad_k, grad_v)


def pair_block(block_text, pair_image, first_caption, keys, values, first_image):
    count = block_text.shape[0]
    width = block_text.shape[1]
    text_wide = block_text.astype(jnp.float32)
    tnorm = lax.rsqrt(jnp.mean(text_wide * text_wide, -1, keepdims=True) + EPS)
    normed = text_wide * tnorm
    pairs = lax.dynamic_slice_in_dim(pair_image, first_caption, count)
    image_ids = first_image + jnp.arange(keys.shape[0], dtype=jnp.int32)

    def one_image(carry, item):
        keys_one, values_one, image_id = item
        loss, grad_x, grad_k, grad_v = image_terms(
            block_text, normed, tnorm, pairs, image_id, keys_one, values_one
        )
        return ((carry[0] + loss, carry[1] + grad_x), (grad_k, grad_v))

    start = (jnp.zeros((count,), jnp.float32), jnp.zeros((count, width), jnp.float32))
    (loss_sum, grad_text), (grad_keys, grad_values) = lax.scan(
        one_image, start, (keys, values, image_ids)
    )
    return (loss_sum, grad_text, grad_keys, grad_values)


def local(text, keys, values, pair_image):
    per_device = keys.shape[0]
    groups = lax.axis_size("blk")
    members = lax.axis_size("grp")
    group_index = lax.axis_index("blk")
    first_image = (group_index * members + lax.axis_index("grp")) * per_device
    image_total = per_device * groups * members
    group_text = lax.all_gather(text, "grp", axis=0, tiled=True)
    span = group_text.shape[0]
    carried = (jnp.zeros((span,), jnp.float32), jnp.zeros((span, text.shape[1]), jnp.float32))
    grad_keys = jnp.zeros(keys.shape, jnp.float32)
    grad_values = jnp.zeros(values.shape, jnp.float32)
    for turn in range(groups):
        source = (group_index - turn) % groups
        loss_part, grad_part, keys_part, values_part = pair_block(
            group_text, pair_image, source * span, keys, values, first_image
        )
        carried = (carried[0] + loss_part, carried[1] + grad_part)
        grad_keys = grad_keys + keys_part
        grad_values = grad_values + values_part
        if turn + 1 < groups:
            group_text = passed_along(group_text, "blk", 1)
        carried = passed_along((carried[0], carried[1]), "blk", 1)
    loss_own, grad_own = (
        lax.psum_scatter(carried[0], "grp", scatter_dimension=0, tiled=True),
        lax.psum_scatter(carried[1], "grp", scatter_dimension=0, tiled=True),
    )
    return (loss_own / image_total, grad_own, grad_keys, grad_values)


def solution(mesh):
    placed = (
        P(("blk", "grp"), None),
        P(("blk", "grp"), None, None),
        P(("blk", "grp"), None, None),
        P(),
    )
    return jax.shard_map(
        local,
        mesh=mesh,
        in_specs=placed,
        out_specs=(
            P(("blk", "grp")),
            P(("blk", "grp"), None),
            P(("blk", "grp"), None, None),
            P(("blk", "grp"), None, None),
        ),
        check_vma=False,
    )
```

profile of v0, /device:TPU:0, one launch (start us, length us, event | category | flops | bytes accessed | tf_op | source)
XLA Modules:
  0.0 104.7 jit_solution(5783523239401266928)
XLA Ops:
  0.6 28.1 %all-gather = bf16[8,1,512]{2,1,0:T(2,128)(2,1)S(1)} all-gather(bf16[1,1,512]{2,1,0:T(2,128)(2,1)} %bitcast.91), channel_id=1, replica_groups=mesh['blk'=4,'grp'=8] {'grp'}, dimensions={0}, use_global_device_ids=true | all-gather | bytes 9216 | tf_op jit(solution)/shard_map/all_gather | solution.py:92
  28.7 0.1 fusion.102
  28.9 1.1 %copy.92 = bf16[1,196,512]{1,2,0:T(8,128)(2,1)S(1)} copy(bf16[1,196,512]{2,1,0:T(8,128)(2,1)} %param.6) | data formatting | bytes 401408 | tf_op args[2]
  30.0 0.1 copy.90
  30.3 0.1 fusion.31
  30.4 1.3 %fusion.180 = (f32[8,8]{0,1:T(8,128)S(1)}, f32[8,8,196]{2,0,1:T(8,128)S(1)}) fusion(f32[8,8,196]{2,0,1:T(8,128)S(1)} %fusion.31), kind=kOutput, calls=%fused_computation.247 | output fusion | flops 25283 | bytes 100608 | tf_op jit(solution)/shard_map/while/body/eval_jaxpr/sub | solution.py:28
  31.8 0.4 multiply_reduce_fusion.7
  32.3 0.2 fusion.97
  32.5 0.5 copy-done.1
  33.0 1.6 %collective-permute-start = (f32[8]{0:T(128)S(1)}, f32[8]{0:T(128)S(1)}, u32[]{:S(2)}, u32[]{:S(2)}) collective-permute-start(f32[8]{0:T(128)S(1)} %compare_select_fusion.3), channel_id=1, source_target_pairs={{24,0},{0,8},{8,16},{16,24},{25,1},{1,9},{9,17},{17,25},{26,2},{2,... | collective-permute-start | bytes 104 | tf_op jit(solution)/shard_map/ppermute | solution.py:15
  34.7 0.2 fusion.98
  34.9 0.1 reshape.340
  35.0 0.1 convolution_bitcast_fusion.3
  35.2 0.3 convolution_bitcast_fusion.7
  35.7 0.4 fusion.36
  36.1 0.3 fusion.130
  36.6 0.6 copy-done.2
  37.2 0.6 dynamic-slice
  37.9 0.1 fusion.30
  38.0 1.3 %fusion.179 = (f32[8,8]{0,1:T(8,128)S(1)}, f32[8,8,196]{2,0,1:T(8,128)S(1)}) fusion(f32[8,8,196]{2,0,1:T(8,128)S(1)} %fusion.30), kind=kOutput, calls=%fused_computation.246 | output fusion | flops 25283 | bytes 100608 | tf_op jit(solution)/shard_map/while/body/eval_jaxpr/sub | solution.py:28
  39.3 0.4 multiply_reduce_fusion.6
  39.8 0.1 fusion.109
  40.0 0.2 fusion.103
  40.2 0.1 fusion.165
  40.3 0.7 collective-permute-start.2
  40.9 0.2 fusion.104
  41.2 0.1 reshape.342
  41.3 0.1 convolution_bitcast_fusion.2
  41.5 0.3 convolution_bitcast_fusion.6
  41.8 0.4 convolution_add_fusion.5
  42.2 0.3 convolution_add_fusion.2
  42.7 3.0 %collective-permute-done.3 = bf16[8,512]{1,0:T(8,128)(2,1)S(1)} collective-permute-done((bf16[8,512]{1,0:T(8,128)(2,1)S(1)}, bf16[8,512]{1,0:T(8,128)(2,1)S(1)}, u32[]{:S(2)}, u32[]{:S(2)}) %collective-permute-start.3) | collective-permute-done | bytes 8224 | tf_op jit(solution)/shard_map/ppermute | solution.py:15
  45.8 0.1 fusion.29
  45.9 1.3 %fusion.178 = (f32[8,8]{0,1:T(8,128)S(1)}, f32[8,8,196]{2,0,1:T(8,128)S(1)}) fusion(f32[8,8,196]{2,0,1:T(8,128)S(1)} %fusion.29), kind=kOutput, calls=%fused_computation.245 | output fusion | flops 25283 | bytes 100608 | tf_op jit(solution)/shard_map/while/body/eval_jaxpr/sub | solution.py:28
  47.2 0.4 multiply_reduce_fusion.5
  47.7 0.1 fusion.116
  47.9 0.2 fusion.110
  48.1 0.1 fusion.166
  48.3 1.6 %collective-permute-start.8 = (f32[8,512]{1,0:T(8,128)S(1)}, f32[8,512]{1,0:T(8,128)S(1)}, u32[]{:S(2)}, u32[]{:S(2)}) collective-permute-start(f32[8,512]{1,0:T(8,128)S(1)} %fusion.108), channel_id=1, source_target_pairs={{24,0},{0,8},{8,16},{16,24},{25,1},{1,9},{9,17},{17,25},{26,2},{2,... | collective-permute-start | bytes 49160 | tf_op jit(solution)/shard_map/ppermute | solution.py:15
  49.9 0.2 fusion.111
  50.3 0.1 convolution_bitcast_fusion.1
  50.4 0.3 convolution_bitcast_fusion.5
  50.7 0.4 convolution_add_fusion.4
  51.2 0.3 convolution_add_fusion.1
  51.7 3.0 %collective-permute-done.5 = bf16[8,512]{1,0:T(8,128)(2,1)S(1)} collective-permute-done((bf16[8,512]{1,0:T(8,128)(2,1)S(1)}, bf16[8,512]{1,0:T(8,128)(2,1)S(1)}, u32[]{:S(2)}, u32[]{:S(2)}) %collective-permute-start.5) | collective-permute-done | bytes 8224 | tf_op jit(solution)/shard_map/ppermute | solution.py:15
  54.7 0.1 fusion.28
  54.9 1.3 %fusion.177 = (f32[8,8]{0,1:T(8,128)S(1)}, f32[8,8,196]{2,0,1:T(8,128)S(1)}) fusion(f32[8,8,196]{2,0,1:T(8,128)S(1)} %fusion.28), kind=kOutput, calls=%fused_computation.244 | output fusion | flops 25283 | bytes 100608 | tf_op jit(solution)/shard_map/while/body/eval_jaxpr/sub | solution.py:28
  56.2 0.4 multiply_reduce_fusion.4
  56.7 0.1 fusion.123
  56.8 0.2 fusion.117
  57.0 0.1 fusion.167
  57.2 0.2 fusion.118
  57.6 0.1 convolution_bitcast_fusion
  57.7 0.4 convolution_add_fusion.3
  58.1 0.3 convolution_bitcast_fusion.4
  58.5 0.6 collective-permute-start.9
  59.3 2.4 %collective-permute-done.9 = f32[8,512]{1,0:T(8,128)S(1)} collective-permute-done((f32[8,512]{1,0:T(8,128)S(1)}, f32[8,512]{1,0:T(8,128)S(1)}, u32[]{:S(2)}, u32[]{:S(2)}) %collective-permute-start.9) | collective-permute-done | bytes 16416 | tf_op jit(solution)/shard_map/ppermute | solution.py:15
  61.8 0.3 convolution_add_fusion
  62.1 1.0 copy.116
  63.2 1.0 copy.117
  64.2 0.8 collective-permute-done.10
  65.0 35.4 %all-reduce.2 = (f32[8]{0:T(128)S(1)}, f32[8,512]{1,0:T(8,128)S(1)}) all-reduce(f32[8]{0:T(128)S(1)} %collective-permute-done.6, f32[8,512]{1,0:T(8,128)S(1)} %collective-permute-done.10), channel_id=2, replica_groups=mesh['blk'=4,'grp'=8] {'grp'}, use_global_device_ids=true, to_apply=%region_20.21.clone | all-reduce | flops 4104 | bytes 32832
  100.4 1.3 %dynamic-slice.1 = f32[1]{0:T(128)} dynamic-slice(f32[8]{0:T(128)S(1)} %get-tuple-element.148, u32[]{:T(128)} %bitcast.23), dynamic_slice_sizes={1} | dynamic-slice | bytes 12
  101.7 1.2 %constant_dynamic-slice_fusion = f32[1,512]{1,0:T(1,128)} fusion(f32[8,512]{1,0:T(8,128)S(1)} %get-tuple-element.149, u32[]{:T(128)} %bitcast.23), kind=kLoop, calls=%fused_computation.211 | loop fusion | bytes 4100
  (65 shorter events, 2.5 us)
Async XLA Ops:
  28.8 9.0 %collective-permute-start.1 = (bf16[8,512]{1,0:T(8,128)(2,1)S(1)}, bf16[8,512]{1,0:T(8,128)(2,1)S(1)}, u32[]{:S(2)}, u32[]{:S(2)}) collective-permute-start(bf16[8,512]{1,0:T(8,128)(2,1)S(1)} %get-tuple-element.153), channel_id=1, source_target_pairs={{24,0},{0,8},{8,16},{16,24},{25,1},{1,9},{9,17},{17,25},{26,2},{2,... | collective-permute-start | bytes 24584 | tf_op jit(solution)/shard_map/ppermute | solution.py:15
  28.9 1.1 %copy-start = (bf16[1,196,512]{2,1,0:T(8,128)(2,1)S(1)}, bf16[1,196,512]{2,1,0:T(8,128)(2,1)}, u32[]{:S(2)}) copy-start(bf16[1,196,512]{2,1,0:T(8,128)(2,1)} %param.5) | copy-start | bytes 602116
  32.3 0.7 copy-start.1
  33.0 7.1 %collective-permute-start = (f32[8]{0:T(128)S(1)}, f32[8]{0:T(128)S(1)}, u32[]{:S(2)}, u32[]{:S(2)}) collective-permute-start(f32[8]{0:T(128)S(1)} %compare_select_fusion.3), channel_id=1, source_target_pairs={{24,0},{0,8},{8,16},{16,24},{25,1},{1,9},{9,17},{17,25},{26,2},{2,... | collective-permute-start | bytes 104 | tf_op jit(solution)/shard_map/ppermute | solution.py:15
  35.7 12.5 %collective-permute-start.7 = (f32[8,512]{1,0:T(8,128)S(1)}, f32[8,512]{1,0:T(8,128)S(1)}, u32[]{:S(2)}, u32[]{:S(2)}) collective-permute-start(f32[8,512]{1,0:T(8,128)S(1)} %fusion.101), channel_id=1, source_target_pairs={{24,0},{0,8},{8,16},{16,24},{25,1},{1,9},{9,17},{17,25},{26,2},{2,... | collective-permute-start | bytes 49160 | tf_op jit(solution)/shard_map/ppermute | solution.py:15
  36.6 0.7 copy-start.2
  40.3 7.8 %collective-permute-start.2 = (f32[8]{0:T(128)S(1)}, f32[8]{0:T(128)S(1)}, u32[]{:S(2)}, u32[]{:S(2)}) collective-permute-start(f32[8]{0:T(128)S(1)} %get-tuple-element.171), channel_id=1, source_target_pairs={{24,0},{0,8},{8,16},{16,24},{25,1},{1,9},{9,17},{17,25},{26,2},{2,... | collective-permute-start | bytes 104 | tf_op jit(solution)/shard_map/ppermute | solution.py:15
  42.6 3.1 %collective-permute-start.3 = (bf16[8,512]{1,0:T(8,128)(2,1)S(1)}, bf16[8,512]{1,0:T(8,128)(2,1)S(1)}, u32[]{:S(2)}, u32[]{:S(2)}) collective-permute-start(bf16[8,512]{1,0:T(8,128)(2,1)S(1)} %collective-permute-done.1), channel_id=1, source_target_pairs={{24,0},{0,8},{8,16},{16,24},{25,1},{1,9},{9,17},{17,25},{26,2},{2,... | collective-permute-start | bytes 24584 | tf_op jit(solution)/shard_map/ppermute | solution.py:15
  48.2 8.9 %collective-permute-start.4 = (f32[8]{0:T(128)S(1)}, f32[8]{0:T(128)S(1)}, u32[]{:S(2)}, u32[]{:S(2)}) collective-permute-start(f32[8]{0:T(128)S(1)} %get-tuple-element.169), channel_id=1, source_target_pairs={{24,0},{0,8},{8,16},{16,24},{25,1},{1,9},{9,17},{17,25},{26,2},{2,... | collective-permute-start | bytes 104 | tf_op jit(solution)/shard_map/ppermute | solution.py:15
  48.3 10.1 %collective-permute-start.8 = (f32[8,512]{1,0:T(8,128)S(1)}, f32[8,512]{1,0:T(8,128)S(1)}, u32[]{:S(2)}, u32[]{:S(2)}) collective-permute-start(f32[8,512]{1,0:T(8,128)S(1)} %fusion.108), channel_id=1, source_target_pairs={{24,0},{0,8},{8,16},{16,24},{25,1},{1,9},{9,17},{17,25},{26,2},{2,... | collective-permute-start | bytes 49160 | tf_op jit(solution)/shard_map/ppermute | solution.py:15
  51.5 3.1 %collective-permute-start.5 = (bf16[8,512]{1,0:T(8,128)(2,1)S(1)}, bf16[8,512]{1,0:T(8,128)(2,1)S(1)}, u32[]{:S(2)}, u32[]{:S(2)}) collective-permute-start(bf16[8,512]{1,0:T(8,128)(2,1)S(1)} %collective-permute-done.3), channel_id=1, source_target_pairs={{24,0},{0,8},{8,16},{16,24},{25,1},{1,9},{9,17},{17,25},{26,2},{2,... | collective-permute-start | bytes 24584 | tf_op jit(solution)/shard_map/ppermute | solution.py:15
  57.1 7.0 %collective-permute-start.6 = (f32[8]{0:T(128)S(1)}, f32[8]{0:T(128)S(1)}, u32[]{:S(2)}, u32[]{:S(2)}) collective-permute-start(f32[8]{0:T(128)S(1)} %get-tuple-element.155), channel_id=1, source_target_pairs={{24,0},{0,8},{8,16},{16,24},{25,1},{1,9},{9,17},{17,25},{26,2},{2,... | collective-permute-start | bytes 104 | tf_op jit(solution)/shard_map/ppermute | solution.py:15
  58.5 3.2 %collective-permute-start.9 = (f32[8,512]{1,0:T(8,128)S(1)}, f32[8,512]{1,0:T(8,128)S(1)}, u32[]{:S(2)}, u32[]{:S(2)}) collective-permute-start(f32[8,512]{1,0:T(8,128)S(1)} %fusion.115), channel_id=1, source_target_pairs={{24,0},{0,8},{8,16},{16,24},{25,1},{1,9},{9,17},{17,25},{26,2},{2,... | collective-permute-start | bytes 49160 | tf_op jit(solution)/shard_map/ppermute | solution.py:15
  61.8 3.2 %collective-permute-start.10 = (f32[8,512]{1,0:T(8,128)S(1)}, f32[8,512]{1,0:T(8,128)S(1)}, u32[]{:S(2)}, u32[]{:S(2)}) collective-permute-start(f32[8,512]{1,0:T(8,128)S(1)} %fusion.122), channel_id=1, source_target_pairs={{24,0},{0,8},{8,16},{16,24},{25,1},{1,9},{9,17},{17,25},{26,2},{2,... | collective-permute-start | bytes 49160 | tf_op jit(solution)/shard_map/ppermute | solution.py:15
where the time goes:
time: 105 us
  blocking collectives  63.5 us (60%)
  waiting for transfers between devices  9.17 us (9%)
  local copies, waits for them, and re-layouts  8.86 us (8%)
  other arithmetic  8.36 us (8%)
  matrix products  7.13 us (7%)
  starting transfers between devices  4.88 us (5%)
  between operations  2.85 us (3%)
    unnamed x1, blocking collectives  35.4 us
    all_gather x1, blocking collectives, local(): group_text = lax.all_gather(text, 'grp', axis=0, tiled=True)  28.1 us
    ppermute x11, waiting for transfers between devices, passed_along(): return lax.ppermute(block, axis, route)  9.17 us
    unnamed x13, local copies, waits for them, and re-layouts  7.48 us
    sub x4, other arithmetic, image_terms(): weights = jax.nn.softmax(scores, axis=-1)  5.22 us
    ppermute x11, starting transfers between devices, passed_along(): return lax.ppermute(block, axis, route)  4.88 us
  transfers between devices with their start and end apart: 11, of which 4 were waited for; matrix products, arithmetic and copies ran while one was open for 20% of the time, Pallas kernels for 0%

commit v1 on v0

--- a/solution.py
+++ b/solution.py
@@ -89,7 +89,14 @@
     group_index = lax.axis_index("blk")
     first_image = (group_index * members + lax.axis_index("grp")) * per_device
     image_total = per_device * groups * members
-    group_text = lax.all_gather(text, "grp", axis=0, tiled=True)
+    size = lax.axis_size("grp")
+    forward = [(i_2, (i_2 + 1) % size) for i_2 in range(size)]
+    parts = [text]
+    for far in range(1, size):
+        parts = [lax.ppermute(parts[0], "grp", forward), *parts]
+    whole = jnp.concatenate(parts, axis=0)
+    places = (lax.axis_index("grp") + 1) * parts[-1].shape[0]
+    group_text = jnp.roll(whole, places, axis=0)
     span = group_text.shape[0]
     carried = (jnp.zeros((span,), jnp.float32), jnp.zeros((span, text.shape[1]), jnp.float32))
     grad_keys = jnp.zeros(keys.shape, jnp.float32)

time: 105 us -> 117 us (1.11)
  waiting for transfers between devices: 9.17 us -> 44.5 us
  blocking collectives: 63.5 us -> 33.9 us
  starting transfers between devices: 4.88 us -> 10.9 us
    ppermute x0 -> x7, waiting for transfers between devices: none -> 39.9 us  [local(): parts = [lax.ppermute(parts[0], 'grp', forward), *parts]]
    all_gather x1 -> x0, blocking collectives: 28.1 us -> none  [local(): group_text = lax.all_gather(text, 'grp', axis=0, tiled=True)]
    ppermute x11, waiting for transfers between devices: 9.17 us -> 4.61 us  [passed_along(): return lax.ppermute(block, axis, route)]
    ppermute x0 -> x7, starting transfers between devices: none -> 3.06 us  [local(): parts = [lax.ppermute(parts[0], 'grp', forward), *parts]]
    ppermute x11, starting transfers between devices: 4.88 us -> 7.82 us  [passed_along(): return lax.ppermute(block, axis, route)]
    unnamed x1, blocking collectives: 35.4 us -> 33.9 us
    unnamed x13 -> x15, local copies, waits for them, and re-layouts: 7.48 us -> 7.49 us
  transfers between devices with their start and end apart: 11 -> 18, of which waited for: 4 -> 11; matrix products, arithmetic and copies ran while one was open for 20% -> 18% of each run, Pallas kernels for 0% -> 0%
where the time goes in v1:
time: 117 us
  waiting for transfers between devices  44.5 us (38%)
  blocking collectives  33.9 us (29%)
  starting transfers between devices  10.9 us (9%)
  local copies, waits for them, and re-layouts  8.94 us (8%)
  other arithmetic  8.34 us (7%)
  matrix products  7.12 us (6%)
  between operations  2.81 us (2%)
    ppermute x7, waiting for transfers between devices, local(): parts = [lax.ppermute(parts[0], 'grp', forward), *parts]  39.9 us
    unnamed x1, blocking collectives  33.9 us
    ppermute x11, starting transfers between devices, passed_along(): return lax.ppermute(block, axis, route)  7.82 us
    unnamed x15, local copies, waits for them, and re-layouts  7.49 us
    sub x4, other arithmetic, image_terms(): weights = jax.nn.softmax(scores, axis=-1)  5.22 us
    ppermute x11, waiting for transfers between devices, passed_along(): return lax.ppermute(block, axis, route)  4.61 us
    ppermute x7, starting transfers between devices, local(): parts = [lax.ppermute(parts[0], 'grp', forward), *parts]  3.06 us
  transfers between devices with their start and end apart: 18, of which 11 were waited for; matrix products, arithmetic and copies ran while one was open for 18% of the time, Pallas kernels for 0%

profile of v1, /device:TPU:0, one launch (start us, length us, event | category | flops | bytes accessed | tf_op | source)
XLA Modules:
  0.0 116.5 jit_solution(6766127199659232967)
XLA Ops:
  0.6 3.0 %collective-permute-start = (bf16[1,512]{1,0:T(2,128)(2,1)}, bf16[1,512]{1,0:T(2,128)(2,1)S(1)}, u32[]{:S(2)}, u32[]{:S(2)}) collective-permute-start(bf16[1,512]{1,0:T(2,128)(2,1)} %param.4), channel_id=1, source_target_pairs={{0,1},{1,2},{2,3},{3,4},{4,5},{5,6},{6,7},{7,0},{8,9},{9,10},{10,1... | collective-permute-start | bytes 3080 | tf_op jit(solution)/shard_map/ppermute | solution.py:96
  3.7 4.8 %collective-permute-done = bf16[1,512]{1,0:T(2,128)(2,1)S(1)} collective-permute-done((bf16[1,512]{1,0:T(2,128)(2,1)}, bf16[1,512]{1,0:T(2,128)(2,1)S(1)}, u32[]{:S(2)}, u32[]{:S(2)}) %collective-permute-start) | collective-permute-done | bytes 1056 | tf_op jit(solution)/shard_map/ppermute | solution.py:96
  8.5 6.3 %collective-permute-done.1 = bf16[1,512]{1,0:T(2,128)(2,1)S(1)} collective-permute-done((bf16[1,512]{1,0:T(2,128)(2,1)S(1)}, bf16[1,512]{1,0:T(2,128)(2,1)S(1)}, u32[]{:S(2)}, u32[]{:S(2)}) %collective-permute-start.1) | collective-permute-done | bytes 1056 | tf_op jit(solution)/shard_map/ppermute | solution.py:96
  14.8 6.3 %collective-permute-done.2 = bf16[1,512]{1,0:T(2,128)(2,1)S(1)} collective-permute-done((bf16[1,512]{1,0:T(2,128)(2,1)S(1)}, bf16[1,512]{1,0:T(2,128)(2,1)S(1)}, u32[]{:S(2)}, u32[]{:S(2)}) %collective-permute-start.2) | collective-permute-done | bytes 1056 | tf_op jit(solution)/shard_map/ppermute | solution.py:96
  21.1 6.3 %collective-permute-done.3 = bf16[1,512]{1,0:T(2,128)(2,1)S(1)} collective-permute-done((bf16[1,512]{1,0:T(2,128)(2,1)S(1)}, bf16[1,512]{1,0:T(2,128)(2,1)S(1)}, u32[]{:S(2)}, u32[]{:S(2)}) %collective-permute-start.3) | collective-permute-done | bytes 1056 | tf_op jit(solution)/shard_map/ppermute | solution.py:96
  27.3 6.3 %collective-permute-done.4 = bf16[1,512]{1,0:T(2,128)(2,1)S(1)} collective-permute-done((bf16[1,512]{1,0:T(2,128)(2,1)S(1)}, bf16[1,512]{1,0:T(2,128)(2,1)S(1)}, u32[]{:S(2)}, u32[]{:S(2)}) %collective-permute-start.4) | collective-permute-done | bytes 1056 | tf_op jit(solution)/shard_map/ppermute | solution.py:96
  33.6 6.3 %collective-permute-done.5 = bf16[1,512]{1,0:T(2,128)(2,1)S(1)} collective-permute-done((bf16[1,512]{1,0:T(2,128)(2,1)S(1)}, bf16[1,512]{1,0:T(2,128)(2,1)S(1)}, u32[]{:S(2)}, u32[]{:S(2)}) %collective-permute-start.5) | collective-permute-done | bytes 1056 | tf_op jit(solution)/shard_map/ppermute | solution.py:96
  39.9 1.1 copy.73
  41.0 0.1 copy.70
  41.2 0.6 copy-done.3
  41.9 0.6 dynamic-slice
  42.5 3.7 %collective-permute-done.6 = bf16[1,512]{1,0:T(2,128)(2,1)S(1)} collective-permute-done((bf16[1,512]{1,0:T(2,128)(2,1)S(1)}, bf16[1,512]{1,0:T(2,128)(2,1)S(1)}, u32[]{:S(2)}, u32[]{:S(2)}) %collective-permute-start.6) | collective-permute-done | bytes 1056 | tf_op jit(solution)/shard_map/ppermute | solution.py:96
  46.3 0.1 fusion.102
  46.5 0.1 fusion.31
  46.7 1.3 %fusion.180 = (f32[8,8]{0,1:T(8,128)S(1)}, f32[8,8,196]{2,0,1:T(8,128)S(1)}) fusion(f32[8,8,196]{2,0,1:T(8,128)S(1)} %fusion.31), kind=kOutput, calls=%fused_computation.247 | output fusion | flops 25283 | bytes 100608 | tf_op jit(solution)/shard_map/while/body/eval_jaxpr/sub | solution.py:28
  48.0 0.4 multiply_reduce_fusion.7
  48.5 0.2 fusion.97
  48.7 0.5 copy-done.2
  49.2 0.2 fusion.98
  49.6 0.1 convolution_bitcast_fusion.3
  49.8 0.3 fusion.130
  50.2 1.8 %collective-permute-start.7 = (f32[8]{0:T(128)S(1)}, f32[8]{0:T(128)S(1)}, u32[]{:S(2)}, u32[]{:S(2)}) collective-permute-start(f32[8]{0:T(128)S(1)} %compare_select_fusion.3), channel_id=1, source_target_pairs={{24,0},{0,8},{8,16},{16,24},{25,1},{1,9},{9,17},{17,25},{26,2},{2,... | collective-permute-start | bytes 104 | tf_op jit(solution)/shard_map/ppermute | solution.py:15
  52.0 0.3 convolution_bitcast_fusion.7
  52.6 0.1 fusion.30
  52.7 1.3 %fusion.179 = (f32[8,8]{0,1:T(8,128)S(1)}, f32[8,8,196]{2,0,1:T(8,128)S(1)}) fusion(f32[8,8,196]{2,0,1:T(8,128)S(1)} %fusion.30), kind=kOutput, calls=%fused_computation.246 | output fusion | flops 25283 | bytes 100608 | tf_op jit(solution)/shard_map/while/body/eval_jaxpr/sub | solution.py:28
  54.0 0.4 multiply_reduce_fusion.6
  54.6 0.2 fusion.103
  54.9 0.2 fusion.104
  55.3 0.1 convolution_bitcast_fusion.2
  55.5 0.3 convolution_bitcast_fusion.6
  55.8 0.4 fusion.36
  56.2 0.5 collective-permute-start.9
  56.7 0.4 convolution_add_fusion.5
  57.2 0.3 convolution_add_fusion.2
  57.7 1.7 %collective-permute-start.15 = (f32[8,512]{1,0:T(8,128)S(1)}, f32[8,512]{1,0:T(8,128)S(1)}, u32[]{:S(2)}, u32[]{:S(2)}) collective-permute-start(f32[8,512]{1,0:T(8,128)S(1)} %fusion.108), channel_id=1, source_target_pairs={{24,0},{0,8},{8,16},{16,24},{25,1},{1,9},{9,17},{17,25},{26,2},{2,... | collective-permute-start | bytes 49160 | tf_op jit(solution)/shard_map/ppermute | solution.py:15
  59.5 1.2 %collective-permute-done.10 = bf16[8,512]{1,0:T(8,128)(2,1)S(1)} collective-permute-done((bf16[8,512]{1,0:T(8,128)(2,1)S(1)}, bf16[8,512]{1,0:T(8,128)(2,1)S(1)}, u32[]{:S(2)}, u32[]{:S(2)}) %collective-permute-start.10) | collective-permute-done | bytes 8224 | tf_op jit(solution)/shard_map/ppermute | solution.py:15
  60.8 0.1 fusion.29
  60.9 1.3 %fusion.178 = (f32[8,8]{0,1:T(8,128)S(1)}, f32[8,8,196]{2,0,1:T(8,128)S(1)}) fusion(f32[8,8,196]{2,0,1:T(8,128)S(1)} %fusion.29), kind=kOutput, calls=%fused_computation.245 | output fusion | flops 25283 | bytes 100608 | tf_op jit(solution)/shard_map/while/body/eval_jaxpr/sub | solution.py:28
  62.2 0.4 multiply_reduce_fusion.5
  62.9 0.2 fusion.110
  63.2 0.2 fusion.111
  63.6 0.1 convolution_bitcast_fusion.1
  63.7 0.3 convolution_bitcast_fusion.5
  64.1 0.4 convolution_add_fusion.4
  64.5 0.3 convolution_add_fusion.1
  64.9 1.8 %collective-permute-start.12 = (bf16[8,512]{1,0:T(8,128)(2,1)S(1)}, bf16[8,512]{1,0:T(8,128)(2,1)S(1)}, u32[]{:S(2)}, u32[]{:S(2)}) collective-permute-start(bf16[8,512]{1,0:T(8,128)(2,1)S(1)} %collective-permute-done.10), channel_id=1, source_target_pairs={{24,0},{0,8},{8,16},{16,24},{25,1},{1,9},{9,17},{17,25},{26,2},{2,... | collective-permute-start | bytes 24584 | tf_op jit(solution)/shard_map/ppermute | solution.py:15
  66.7 1.2 %collective-permute-done.12 = bf16[8,512]{1,0:T(8,128)(2,1)S(1)} collective-permute-done((bf16[8,512]{1,0:T(8,128)(2,1)S(1)}, bf16[8,512]{1,0:T(8,128)(2,1)S(1)}, u32[]{:S(2)}, u32[]{:S(2)}) %collective-permute-start.12) | collective-permute-done | bytes 8224 | tf_op jit(solution)/shard_map/ppermute | solution.py:15
  68.1 0.1 fusion.28
  68.2 1.3 %fusion.177 = (f32[8,8]{0,1:T(8,128)S(1)}, f32[8,8,196]{2,0,1:T(8,128)S(1)}) fusion(f32[8,8,196]{2,0,1:T(8,128)S(1)} %fusion.28), kind=kOutput, calls=%fused_computation.244 | output fusion | flops 25283 | bytes 100608 | tf_op jit(solution)/shard_map/while/body/eval_jaxpr/sub | solution.py:28
  69.5 0.4 multiply_reduce_fusion.4
  70.1 0.2 fusion.117
  70.5 0.2 fusion.118
  70.9 0.1 convolution_bitcast_fusion
  71.0 0.4 convolution_add_fusion.3
  71.5 0.3 convolution_bitcast_fusion.4
  71.9 1.8 %collective-permute-start.16 = (f32[8,512]{1,0:T(8,128)S(1)}, f32[8,512]{1,0:T(8,128)S(1)}, u32[]{:S(2)}, u32[]{:S(2)}) collective-permute-start(f32[8,512]{1,0:T(8,128)S(1)} %fusion.115), channel_id=1, source_target_pairs={{24,0},{0,8},{8,16},{16,24},{25,1},{1,9},{9,17},{17,25},{26,2},{2,... | collective-permute-start | bytes 49160 | tf_op jit(solution)/shard_map/ppermute | solution.py:15
  73.7 1.3 %collective-permute-done.16 = f32[8,512]{1,0:T(8,128)S(1)} collective-permute-done((f32[8,512]{1,0:T(8,128)S(1)}, f32[8,512]{1,0:T(8,128)S(1)}, u32[]{:S(2)}, u32[]{:S(2)}) %collective-permute-start.16) | collective-permute-done | bytes 16416 | tf_op jit(solution)/shard_map/ppermute | solution.py:15
  75.1 0.3 convolution_add_fusion
  75.5 1.0 copy.100
  76.5 1.0 copy.101
  77.5 0.8 collective-permute-done.17
  78.3 33.9 %all-reduce.2 = (f32[8]{0:T(128)S(1)}, f32[8,512]{1,0:T(8,128)S(1)}) all-reduce(f32[8]{0:T(128)S(1)} %collective-permute-done.13, f32[8,512]{1,0:T(8,128)S(1)} %collective-permute-done.17), channel_id=2, replica_groups=mesh['blk'=4,'grp'=8] {'grp'}, use_global_device_ids=true, to_apply=%region_20.21.clone | all-reduce | flops 4104 | bytes 32832
  112.2 1.3 %dynamic-slice.1 = f32[1]{0:T(128)} dynamic-slice(f32[8]{0:T(128)S(1)} %get-tuple-element.144, u32[]{:T(128)} %bitcast.22), dynamic_slice_sizes={1} | dynamic-slice | bytes 12
  113.5 1.2 %constant_dynamic-slice_fusion = f32[1,512]{1,0:T(1,128)} fusion(f32[8,512]{1,0:T(8,128)S(1)} %get-tuple-element.145, u32[]{:T(128)} %bitcast.22), kind=kLoop, calls=%fused_computation.210 | loop fusion | bytes 4100
  (80 shorter events, 3.2 us)
Async XLA Ops:
  0.6 7.9 %collective-permute-start = (bf16[1,512]{1,0:T(2,128)(2,1)}, bf16[1,512]{1,0:T(2,128)(2,1)S(1)}, u32[]{:S(2)}, u32[]{:S(2)}) collective-permute-start(bf16[1,512]{1,0:T(2,128)(2,1)} %param.4), channel_id=1, source_target_pairs={{0,1},{1,2},{2,3},{3,4},{4,5},{5,6},{6,7},{7,0},{8,9},{9,10},{10,1... | collective-permute-start | bytes 3080 | tf_op jit(solution)/shard_map/ppermute | solution.py:96
  8.5 6.3 %collective-permute-start.1 = (bf16[1,512]{1,0:T(2,128)(2,1)S(1)}, bf16[1,512]{1,0:T(2,128)(2,1)S(1)}, u32[]{:S(2)}, u32[]{:S(2)}) collective-permute-start(bf16[1,512]{1,0:T(2,128)(2,1)S(1)} %collective-permute-done), channel_id=1, source_target_pairs={{0,1},{1,2},{2,3},{3,4},{4,5},{5,6},{6,7},{7,0},{8,9},{9,10},{10,1... | collective-permute-start | bytes 3080 | tf_op jit(solution)/shard_map/ppermute | solution.py:96
  14.8 6.3 %collective-permute-start.2 = (bf16[1,512]{1,0:T(2,128)(2,1)S(1)}, bf16[1,512]{1,0:T(2,128)(2,1)S(1)}, u32[]{:S(2)}, u32[]{:S(2)}) collective-permute-start(bf16[1,512]{1,0:T(2,128)(2,1)S(1)} %collective-permute-done.1), channel_id=1, source_target_pairs={{0,1},{1,2},{2,3},{3,4},{4,5},{5,6},{6,7},{7,0},{8,9},{9,10},{10,1... | collective-permute-start | bytes 3080 | tf_op jit(solution)/shard_map/ppermute | solution.py:96
  21.1 6.3 %collective-permute-start.3 = (bf16[1,512]{1,0:T(2,128)(2,1)S(1)}, bf16[1,512]{1,0:T(2,128)(2,1)S(1)}, u32[]{:S(2)}, u32[]{:S(2)}) collective-permute-start(bf16[1,512]{1,0:T(2,128)(2,1)S(1)} %collective-permute-done.2), channel_id=1, source_target_pairs={{0,1},{1,2},{2,3},{3,4},{4,5},{5,6},{6,7},{7,0},{8,9},{9,10},{10,1... | collective-permute-start | bytes 3080 | tf_op jit(solution)/shard_map/ppermute | solution.py:96
  27.3 6.3 %collective-permute-start.4 = (bf16[1,512]{1,0:T(2,128)(2,1)S(1)}, bf16[1,512]{1,0:T(2,128)(2,1)S(1)}, u32[]{:S(2)}, u32[]{:S(2)}) collective-permute-start(bf16[1,512]{1,0:T(2,128)(2,1)S(1)} %collective-permute-done.3), channel_id=1, source_target_pairs={{0,1},{1,2},{2,3},{3,4},{4,5},{5,6},{6,7},{7,0},{8,9},{9,10},{10,1... | collective-permute-start | bytes 3080 | tf_op jit(solution)/shard_map/ppermute | solution.py:96
  33.6 6.3 %collective-permute-start.5 = (bf16[1,512]{1,0:T(2,128)(2,1)S(1)}, bf16[1,512]{1,0:T(2,128)(2,1)S(1)}, u32[]{:S(2)}, u32[]{:S(2)}) collective-permute-start(bf16[1,512]{1,0:T(2,128)(2,1)S(1)} %collective-permute-done.4), channel_id=1, source_target_pairs={{0,1},{1,2},{2,3},{3,4},{4,5},{5,6},{6,7},{7,0},{8,9},{9,10},{10,1... | collective-permute-start | bytes 3080 | tf_op jit(solution)/shard_map/ppermute | solution.py:96
  39.9 6.3 %collective-permute-start.6 = (bf16[1,512]{1,0:T(2,128)(2,1)S(1)}, bf16[1,512]{1,0:T(2,128)(2,1)S(1)}, u32[]{:S(2)}, u32[]{:S(2)}) collective-permute-start(bf16[1,512]{1,0:T(2,128)(2,1)S(1)} %collective-permute-done.5), channel_id=1, source_target_pairs={{0,1},{1,2},{2,3},{3,4},{4,5},{5,6},{6,7},{7,0},{8,9},{9,10},{10,1... | collective-permute-start | bytes 3080 | tf_op jit(solution)/shard_map/ppermute | solution.py:96
  39.9 1.1 copy-start
  41.2 5.0 %copy-start.1 = (bf16[1,512]{1,0:T(2,128)(2,1)S(1)}, bf16[1,512]{1,0:T(2,128)(2,1)}, u32[]{:S(2)}) copy-start(bf16[1,512]{1,0:T(2,128)(2,1)} %param.4) | copy-start | bytes 3076
  41.2 0.7 copy-start.3
  46.4 6.1 %collective-permute-start.8 = (bf16[8,512]{1,0:T(8,128)(2,1)S(1)}, bf16[8,512]{1,0:T(8,128)(2,1)S(1)}, u32[]{:S(2)}, u32[]{:S(2)}) collective-permute-start(bf16[8,512]{1,0:T(8,128)(2,1)S(1)} %get-tuple-element.149), channel_id=1, source_target_pairs={{24,0},{0,8},{8,16},{16,24},{25,1},{1,9},{9,17},{17,25},{26,2},{2,... | collective-permute-start | bytes 24584 | tf_op jit(solution)/shard_map/ppermute | solution.py:15
  48.5 0.7 copy-start.2
  50.2 4.7 %collective-permute-start.7 = (f32[8]{0:T(128)S(1)}, f32[8]{0:T(128)S(1)}, u32[]{:S(2)}, u32[]{:S(2)}) collective-permute-start(f32[8]{0:T(128)S(1)} %compare_select_fusion.3), channel_id=1, source_target_pairs={{24,0},{0,8},{8,16},{16,24},{25,1},{1,9},{9,17},{17,25},{26,2},{2,... | collective-permute-start | bytes 104 | tf_op jit(solution)/shard_map/ppermute | solution.py:15
  52.4 5.2 %collective-permute-start.14 = (f32[8,512]{1,0:T(8,128)S(1)}, f32[8,512]{1,0:T(8,128)S(1)}, u32[]{:S(2)}, u32[]{:S(2)}) collective-permute-start(f32[8,512]{1,0:T(8,128)S(1)} %fusion.101), channel_id=1, source_target_pairs={{24,0},{0,8},{8,16},{16,24},{25,1},{1,9},{9,17},{17,25},{26,2},{2,... | collective-permute-start | bytes 49160 | tf_op jit(solution)/shard_map/ppermute | solution.py:15
  56.2 6.8 %collective-permute-start.9 = (f32[8]{0:T(128)S(1)}, f32[8]{0:T(128)S(1)}, u32[]{:S(2)}, u32[]{:S(2)}) collective-permute-start(f32[8]{0:T(128)S(1)} %get-tuple-element.155), channel_id=1, source_target_pairs={{24,0},{0,8},{8,16},{16,24},{25,1},{1,9},{9,17},{17,25},{26,2},{2,... | collective-permute-start | bytes 104 | tf_op jit(solution)/shard_map/ppermute | solution.py:15
  57.6 3.1 %collective-permute-start.10 = (bf16[8,512]{1,0:T(8,128)(2,1)S(1)}, bf16[8,512]{1,0:T(8,128)(2,1)S(1)}, u32[]{:S(2)}, u32[]{:S(2)}) collective-permute-start(bf16[8,512]{1,0:T(8,128)(2,1)S(1)} %collective-permute-done.8), channel_id=1, source_target_pairs={{24,0},{0,8},{8,16},{16,24},{25,1},{1,9},{9,17},{17,25},{26,2},{2,... | collective-permute-start | bytes 24584 | tf_op jit(solution)/shard_map/ppermute | solution.py:15
  57.7 14.1 %collective-permute-start.15 = (f32[8,512]{1,0:T(8,128)S(1)}, f32[8,512]{1,0:T(8,128)S(1)}, u32[]{:S(2)}, u32[]{:S(2)}) collective-permute-start(f32[8,512]{1,0:T(8,128)S(1)} %fusion.108), channel_id=1, source_target_pairs={{24,0},{0,8},{8,16},{16,24},{25,1},{1,9},{9,17},{17,25},{26,2},{2,... | collective-permute-start | bytes 49160 | tf_op jit(solution)/shard_map/ppermute | solution.py:15
  63.2 7.2 %collective-permute-start.11 = (f32[8]{0:T(128)S(1)}, f32[8]{0:T(128)S(1)}, u32[]{:S(2)}, u32[]{:S(2)}) collective-permute-start(f32[8]{0:T(128)S(1)} %get-tuple-element.153), channel_id=1, source_target_pairs={{24,0},{0,8},{8,16},{16,24},{25,1},{1,9},{9,17},{17,25},{26,2},{2,... | collective-permute-start | bytes 104 | tf_op jit(solution)/shard_map/ppermute | solution.py:15
  64.9 3.1 %collective-permute-start.12 = (bf16[8,512]{1,0:T(8,128)(2,1)S(1)}, bf16[8,512]{1,0:T(8,128)(2,1)S(1)}, u32[]{:S(2)}, u32[]{:S(2)}) collective-permute-start(bf16[8,512]{1,0:T(8,128)(2,1)S(1)} %collective-permute-done.10), channel_id=1, source_target_pairs={{24,0},{0,8},{8,16},{16,24},{25,1},{1,9},{9,17},{17,25},{26,2},{2,... | collective-permute-start | bytes 24584 | tf_op jit(solution)/shard_map/ppermute | solution.py:15
  70.4 7.0 %collective-permute-start.13 = (f32[8]{0:T(128)S(1)}, f32[8]{0:T(128)S(1)}, u32[]{:S(2)}, u32[]{:S(2)}) collective-permute-start(f32[8]{0:T(128)S(1)} %get-tuple-element.151), channel_id=1, source_target_pairs={{24,0},{0,8},{8,16},{16,24},{25,1},{1,9},{9,17},{17,25},{26,2},{2,... | collective-permute-start | bytes 104 | tf_op jit(solution)/shard_map/ppermute | solution.py:15
  71.9 3.2 %collective-permute-start.16 = (f32[8,512]{1,0:T(8,128)S(1)}, f32[8,512]{1,0:T(8,128)S(1)}, u32[]{:S(2)}, u32[]{:S(2)}) collective-permute-start(f32[8,512]{1,0:T(8,128)S(1)} %fusion.115), channel_id=1, source_target_pairs={{24,0},{0,8},{8,16},{16,24},{25,1},{1,9},{9,17},{17,25},{26,2},{2,... | collective-permute-start | bytes 49160 | tf_op jit(solution)/shard_map/ppermute | solution.py:15
  75.1 3.2 %collective-permute-start.17 = (f32[8,512]{1,0:T(8,128)S(1)}, f32[8,512]{1,0:T(8,128)S(1)}, u32[]{:S(2)}, u32[]{:S(2)}) collective-permute-start(f32[8,512]{1,0:T(8,128)S(1)} %fusion.122), channel_id=1, source_target_pairs={{24,0},{0,8},{8,16},{16,24},{25,1},{1,9},{9,17},{17,25},{26,2},{2,... | collective-permute-start | bytes 49160 | tf_op jit(solution)/shard_map/ppermute | solution.py:15
